TPU v7x, 512 devices: a whole 4x4x16 slice. The times are simulated.
512 devices in a mesh: dp: 64 (over z, y), mp: 8 (over x, core).
Axes of the slice: x: 4, y: 4, z: 16, core: 2. Of those that a mesh axis runs over, the one named last changes fastest.
Arguments:
- activations: bfloat16 [32768, 2048], P(('dp', 'mp')), may hold values from -400 to 400
- key_value_grads: bfloat16 [2, 32768, 1024], P(None, 'dp', 'mp'), may hold values from -320 to 320
- master_weights: float32 [2048, 2, 1024], P('dp', None, 'mp'), may hold values from -0.125 to 0.125
- first_moment: float32 [2048, 2, 1024], P('dp', None, 'mp'), may hold values from -0.005859375 to 0.005859375
- second_moment: float32 [2048, 2, 1024], P('dp', None, 'mp'), may hold values from 1e-08 to 1e-05
Outputs:
- master_out: float32 [2048, 2, 1024], P('dp', None, 'mp')
- first_out: float32 [2048, 2, 1024], P('dp', None, 'mp')
- second_out: float32 [2048, 2, 1024], P('dp', None, 'mp')
- weights_out: bfloat16 [2048, 2, 1024], P(None, None, 'mp')
All inputs are finite; a program needn't handle non-finite values.
Results may differ from a plain program's by a relative error of at most 0.001.
Values may be sent and summed in bfloat16 or wider, within the bound.
A program may use at most 64 MiB of HBM per device.

v0:
```python
import math

import jax
import jax.numpy as jnp
from jax import lax
from jax.sharding import Mesh
from jax.sharding import PartitionSpec as P

D = 2048
STEP = 8
KV = 1024
MP = ("mp_0", "mp_1")
DP = ("dp_0", "dp_1")
DP_MP = ("dp_0", "dp_1", "mp_0", "mp_1")


beta_first = 0.9
beta_second = 0.95
adam_epsilon = 1e-08
learning_rate = 0.001
weight_decay = 0.1
clip_scale = 0.001


def copy_for_each(x, axis):
    count = lax.axis_size(axis)
    return lax.all_to_all(jnp.broadcast_to(x[None], (count, *x.shape)), axis, 0, 0, tiled=True)


def laid_out(tiles, dim):
    tiles = jnp.moveaxis(tiles, 0, dim)
    lengths = tiles.shape
    return tiles.reshape(*lengths[:dim], lengths[dim] * lengths[dim + 1], *lengths[dim + 2 :])


def gathered_by_axis(x, axes, dim):
    far, near = axes
    leading = copy_for_each(x, far)
    tiles = jnp.swapaxes(copy_for_each(leading, near), 0, 1)
    return laid_out(tiles.reshape(-1, *x.shape), dim)


def cut_along(x, dim, count):
    before, after = (x.shape[:dim], x.shape[dim + 1 :])
    return jnp.moveaxis(x.reshape(*before, count, -1, *after), dim, 0)


def sum_at_owner(x, axis, dim):
    tiles = cut_along(x, dim, lax.axis_size(axis))
    arrived = lax.all_to_all(tiles, axis, split_axis=0, concat_axis=0, tiled=True)
    return arrived.sum(axis=0)


def summed_rows(x, axes, dim):
    far, near = axes
    tiles = cut_along(x, dim, lax.axis_size(far))
    nearer = sum_at_owner(tiles, near, dim + 1)
    arrived = lax.all_to_all(nearer, far, split_axis=0, concat_axis=0, tiled=True)
    return arrived.sum(axis=0)


def over_copies(x, axis):
    everything = copy_for_each(x, axis)
    return jnp.sum(everything, axis=0)


def over_axes(x, axes):
    far, near = axes
    nearer = over_copies(x, near)
    return over_copies(nearer, far)


def gather_axes(x, axes, dim):
    result = x
    for number in range(len(axes) - 1, -1, -1):
        result = lax.all_gather(result, axes[number], axis=dim, tiled=True)
    return result


def on_device(activations, key_value_grads, master_weights, first_moment, second_moment):
    token_count = activations.shape[0] * lax.axis_size(MP) * lax.axis_size(DP)
    partial_sum = jnp.einsum(
        "td,ctk->dck",
        gathered_by_axis(activations, ("mp_0", "mp_1"), 0),
        key_value_grads,
        preferred_element_type=jnp.float32,
    )
    summed = summed_rows(partial_sum, ("dp_0", "dp_1"), 0)
    gradient = summed / token_count
    local_squares = jnp.sum(gradient * gradient)
    total_squares = over_axes(local_squares, (("dp_0", "dp_1"), ("mp_0", "mp_1")))
    grad_norm = jnp.sqrt(total_squares)
    limit = clip_scale * math.sqrt(2.0 * D * KV)
    clip_factor = jnp.minimum(jnp.float32(1.0), limit / (grad_norm + 1e-06))
    clipped = clip_factor * gradient
    first_out = beta_first * first_moment + (1.0 - beta_first) * clipped
    second_out = beta_second * second_moment + (1.0 - beta_second) * clipped * clipped
    first_hat = first_out / (1.0 - beta_first**STEP)
    second_hat = second_out / (1.0 - beta_second**STEP)
    master_out = master_weights - learning_rate * (
        first_hat / (jnp.sqrt(second_hat) + adam_epsilon) + weight_decay * master_weights
    )
    weights_out = gather_axes(master_out.astype(jnp.bfloat16), DP, 0)
    return (master_out, first_out, second_out, weights_out)


def solution(mesh):
    split = Mesh(mesh.devices.reshape(16, 4, 4, 2), ("dp_0", "dp_1", "mp_0", "mp_1"))
    return jax.shard_map(
        on_device,
        mesh=split,
        in_specs=(
            P(DP_MP, None),
            P(None, DP, MP),
            P(DP, None, MP),
            P(DP, None, MP),
            P(DP, None, MP),
        ),
        out_specs=(P(DP, None, MP), P(DP, None, MP), P(DP, None, MP), P(None, None, MP)),
        check_vma=False,
    )
```

profile of v0, /device:TPU:6, one launch (start us, length us, event | category | flops | bytes accessed | tf_op | source)
XLA Modules:
  0.0 227.2 jit_solution(663511004359050502)
XLA Ops:
  7.2 1.1 broadcast_in_dim.8
  8.3 17.6 %all_to_all.32 = bf16[4,64,2048]{2,1,0:T(8,128)(2,1)S(1)} all-to-all(bf16[4,64,2048]{2,1,0:T(8,128)(2,1)S(1)} %broadcast_in_dim.8), channel_id=1, replica_groups=mesh['dp_0'=16,'dp_1'=4,'mp_0'=4,'mp_1'=2] {'mp_0'}, dimensions={0} | all-to-all | bytes 2097152 | tf_op jit(solution)/shard_map/all_to_all | solution.py:27
  25.9 0.3 broadcast_in_dim.9
  26.2 5.4 %all_to_all.33 = bf16[2,4,64,2048]{3,2,1,0:T(8,128)(2,1)S(1)} all-to-all(bf16[2,4,64,2048]{3,2,1,0:T(8,128)(2,1)S(1)} %broadcast_in_dim.9), channel_id=1, replica_groups=mesh['dp_0'=16,'dp_1'=4,'mp_0'=4,'mp_1'=2] {'mp_1'}, dimensions={0} | all-to-all | bytes 4194304 | tf_op jit(solution)/shard_map/all_to_all | solution.py:27
  31.6 0.1 copy.40
  31.7 2.5 %copy.41 = bf16[2048,512]{1,0:T(8,128)(2,1)} copy(bf16[2048,512]{0,1:T(8,128)(2,1)S(1)} %bitcast.18) | data formatting | bytes 4194304 | tf_op jit(solution)/shard_map/td,ctk->dck/dot_general | solution.py:82
  34.3 2.3 %convolution_bitcast_fusion = f32[4,16,32,2,128]{4,2,3,0,1:T(8,128)S(1)} fusion(bf16[16,4,32,512,1]{3,2,4,1,0:T(8,128)(2,1)} %bitcast.19, bf16[2,512,128]{2,1,0:T(8,128)(2,1)S(1)} %copy-done), kind=kOutput, calls=%fused_computation | convolution fusion | flops 536870912 | bytes 4456448 | tf_op jit(solution)/shard_map/td,ctk->dck/dot_general | solution.py:82
  36.6 0.3 copy.42
  36.9 30.9 %all_to_all.34 = f32[4,16,32,2,128]{4,2,3,1,0:T(8,128)S(1)} all-to-all(f32[4,16,32,2,128]{4,2,3,1,0:T(8,128)S(1)} %copy.42), channel_id=1, replica_groups=mesh['dp_0'=16,'dp_1'=4,'mp_0'=4,'mp_1'=2] {'dp_1'}, dimensions={0} | all-to-all | bytes 4194304 | tf_op jit(solution)/shard_map/all_to_all | solution.py:50
  67.8 0.2 reduce_sum.45
  68.0 42.1 %all_to_all.35 = f32[16,32,2,128]{3,1,2,0:T(8,128)S(1)} all-to-all(f32[16,32,2,128]{3,1,2,0:T(8,128)S(1)} %reduce_sum.45), channel_id=1, replica_groups=mesh['dp_0'=16,'dp_1'=4,'mp_0'=4,'mp_1'=2] {'dp_0'}, dimensions={0} | all-to-all | bytes 1048576 | tf_op jit(solution)/shard_map/all_to_all | solution.py:58
  110.2 0.6 multiply_reduce_fusion
  110.8 0.6 broadcast_in_dim.10
  111.4 7.6 %all_to_all.36 = f32[8,1,1]{2,1,0:T(1,128)S(1)} all-to-all(f32[8,1,1]{2,1,0:T(1,128)S(1)} %broadcast_in_dim.10), channel_id=1, replica_groups=mesh['dp_0'=16,'dp_1'=4,'mp_0'=4,'mp_1'=2] {'mp_0','mp_1'}, dimensions={0} | all-to-all | bytes 64 | tf_op jit(solution)/shard_map/all_to_all | solution.py:27
  119.1 0.6 reduce_sum.48
  119.7 0.7 broadcast_in_dim.11
  120.3 23.1 %all_to_all.37 = f32[64,1,1]{2,1,0:T(1,128)S(1)} all-to-all(f32[64,1,1]{2,1,0:T(1,128)S(1)} %broadcast_in_dim.11), channel_id=1, replica_groups=mesh['dp_0'=16,'dp_1'=4,'mp_0'=4,'mp_1'=2] {'dp_0','dp_1'}, dimensions={0} | all-to-all | bytes 512 | tf_op jit(solution)/shard_map/all_to_all | solution.py:27
  143.5 0.7 reduce_sum.49
  145.0 12.6 %all_gather.6 = bf16[128,2,128]{2,1,0:T(2,128)(2,1)} all-gather(bf16[32,2,128]{2,1,0:T(2,128)(2,1)S(1)} %copy.49), channel_id=1, replica_groups=mesh['dp_0'=16,'dp_1'=4,'mp_0'=4,'mp_1'=2] {'dp_1'}, dimensions={0}, use_global_device_ids=true | all-gather | bytes 81920 | tf_op jit(solution)/shard_map/all_gather | solution.py:76
  157.6 0.6 copy.50
  158.2 0.6 copy.51
  158.9 0.6 copy.52
  159.5 58.3 %all-gather.2.cloned.1.call-done = bf16[2048,2,128]{2,1,0:T(2,128)(2,1)} async-done(((bf16[128,2,128]{2,1,0:T(2,128)(2,1)}), bf16[2048,2,128]{2,1,0:T(2,128)(2,1)}) %all-gather.2.cloned.1.call-update) | async-done | bytes 1048592 | tf_op jit(solution)/shard_map/all_gather | solution.py:76
  217.8 2.6 %copy.69 = bf16[2048,2,128]{2,1,0:T(2,128)(2,1)} copy(bf16[2048,2,128]{2,1,0:T(2,128)(2,1)} %all-gather.2.cloned.1.call-done) | data formatting | bytes 2097152
  (13 shorter events, 0.2 us)
Async XLA Ops:
  7.2 27.1 %copy-start = (bf16[2,512,128]{2,1,0:T(8,128)(2,1)S(1)}, bf16[2,512,128]{2,1,0:T(8,128)(2,1)}, u32[]{:S(2)}) copy-start(bf16[2,512,128]{2,1,0:T(8,128)(2,1)} %param.6) | copy-start | bytes 786436
  7.2 210.6 %all-gather.2.cloned.1.call-start = ((), (), s32[]{:S(2)}) async-start(), calls=%async_computation.6 | async-start | bytes 1114112 | tf_op jit(solution)/shard_map/all_gather | solution.py:76
  67.8 77.1 %copy-start.1 = (f32[32,2,128]{2,1,0:T(2,128)S(1)}, f32[32,2,128]{2,1,0:T(2,128)}, u32[]{:S(2)}) copy-start(f32[32,2,128]{2,1,0:T(2,128)} %param.7) | copy-start | bytes 98308
  67.8 77.1 %copy-start.2 = (f32[32,2,128]{2,1,0:T(2,128)S(1)}, f32[32,2,128]{2,1,0:T(2,128)}, u32[]{:S(2)}) copy-start(f32[32,2,128]{2,1,0:T(2,128)} %param.8) | copy-start | bytes 98308
  67.8 77.1 %copy-start.3 = (f32[32,2,128]{2,1,0:T(2,128)S(1)}, f32[32,2,128]{2,1,0:T(2,128)}, u32[]{:S(2)}) copy-start(f32[32,2,128]{2,1,0:T(2,128)} %param.9) | copy-start | bytes 98308
Sparse Core Ops, SparseCore 0:
  157.7 60.0 all-gather.1
where the time goes:
time: 228 us; the launch traced here: 227 us
  blocking collectives  139 us (61%)
  waiting for transfers between devices  58.3 us (26%)
  between operations  14.9 us (7%)
  local copies, waits for them, and re-layouts  10.1 us (4%)
  matrix products  2.3 us (1%)
    all_gather x1, waiting for transfers between devices, gather_axes(): result = lax.all_gather(result, axes[number], axis=dim, tiled=True)  58.3 us
    all_to_all x4, blocking collectives, copy_for_each(): lax.all_to_all(jnp.broadcast_to(x[None], (count, *x.shape)), axis, 0, 0,...  53.8 us
    all_to_all x1, blocking collectives, summed_rows(): lax.all_to_all(nearer, far, split_axis=0, concat_axis=0, tiled=True)  42.1 us
    all_to_all x1, blocking collectives, sum_at_owner(): lax.all_to_all(tiles, axis, split_axis=0, concat_axis=0, tiled=True)  30.9 us
    all_gather x1, blocking collectives, gather_axes(): result = lax.all_gather(result, axes[number], axis=dim, tiled=True)  12.6 us
  transfers between devices with their start and end apart: 1, of which 1 were waited for; matrix products, arithmetic and copies ran while one was open for 1% of the time, Pallas kernels for 0%

commit v1 on v0

v1 whole, which is shorter than its diff:
```python
import math

import jax
import jax.numpy as jnp
from jax import lax
from jax.experimental import pallas as pl
from jax.experimental.pallas import tpu as pltpu
from jax.sharding import Mesh
from jax.sharding import PartitionSpec as P

D = 2048
STEP = 8
KV = 1024
NZ, NY, NX, NC = 16, 4, 4, 2
STEPS = 8
DP = ("z", "y")
MP = ("x", "c")
DP_MP = ("z", "y", "x", "c")
MESH_ID = pl.DeviceIdType.MESH

beta_first = 0.9
beta_second = 0.95
adam_epsilon = 1e-08
learning_rate = 0.001
weight_decay = 0.1
clip_scale = 0.001

GROUP = [(dx, dc) for dc in range(NC) for dx in range(NX) if (dx, dc) != (0, 0)]


def step_kernel(
    acts_hbm, grads_hbm, master_hbm, first_hbm, second_hbm,
    master_out, first_out, second_out, weights_out,
    acts, slabs, cols, part, ysend, yrecv, zsend, zrecv, half, peer_half,
    nsend, nrecv_g, nrecv_y, nrecv_z,
    master, first, second, wide, rows_out, wbuf,
    load_sem, own_sem, grad_sem, state_sem, swap_send, swap_recv,
    xsend_sem, xrecv_sem, ysend_sem, yrecv_sem, zsend_sem, zrecv_sem,
    half_send, half_recv, nsend_sem, nrecv_sem, gsend_sem, gz_sem, gy_sem, out_sem,
):
    z, y, x, c = (lax.axis_index(a) for a in DP_MP)
    dp = z * NY + y
    mp = x * NC + c

    def at_z(k):
        return (lax.rem(z + k, NZ), y, x, c)

    def at_y(k):
        return (z, lax.rem(y + k, NY), x, c)

    def at_group(dx, dc):
        return (z, y, lax.rem(x + dx, NX), lax.rem(c + dc, NC))

    def block_of(i, core):
        return lax.rem(z + jnp.where(core == 0, 8 + i, 7 - i), NZ)

    def send(src, dst, send_sem, recv_sem, device):
        copy = pltpu.make_async_remote_copy(
            src_ref=src, dst_ref=dst, send_sem=send_sem, recv_sem=recv_sem,
            device_id=device, device_id_type=MESH_ID,
        )
        copy.start()

    def wait_bytes(ref, sem):
        pltpu.make_async_copy(ref, ref, sem).wait()

    barrier = pltpu.get_barrier_semaphore()
    for k in range(1, NZ):
        pl.semaphore_signal(barrier, inc=1, device_id=at_z(k), device_id_type=MESH_ID)
    for k in range(1, NY):
        pl.semaphore_signal(barrier, inc=1, device_id=at_y(k), device_id_type=MESH_ID)
    for dx, dc in GROUP:
        pl.semaphore_signal(barrier, inc=1, device_id=at_group(dx, dc), device_id_type=MESH_ID)

    own_rows = pl.ds(pl.multiple_of(mp * 64, 64), 64)
    own_cols = pl.ds(pl.multiple_of(c * 256, 256), 256)
    for b in range(NZ):
        pltpu.make_async_copy(acts_hbm.at[:, pl.ds(b * 128, 128)], acts.at[b], load_sem).start()
    for which in range(2):
        lanes = pl.ds(pl.multiple_of(c * 256 + which * 128, 128), 128)
        pltpu.make_async_copy(grads_hbm.at[which], cols.at[:, lanes], grad_sem).start()
    for i in range(STEPS):
        lanes = pl.ds(pl.multiple_of(block_of(i, c) * 128, 128), 128)
        pltpu.make_async_copy(acts_hbm.at[:, lanes], slabs.at[i, own_rows], own_sem).start()
    pltpu.make_async_copy(master_hbm, master, state_sem.at[0]).start()
    pltpu.make_async_copy(first_hbm, first, state_sem.at[1]).start()
    pltpu.make_async_copy(second_hbm, second, state_sem.at[2]).start()

    wait_bytes(acts, load_sem)
    wait_bytes(cols.at[:, pl.ds(0, 256)], grad_sem)
    pl.semaphore_wait(barrier, (NZ - 1) + (NY - 1) + len(GROUP))

    send(cols.at[:, own_cols], cols.at[:, own_cols], swap_send, swap_recv, at_group(0, 1))

    def gather_step(i, carry):
        for core in range(NC):
            slab = acts.at[block_of(i, core)]
            for dx in range(1, NX):
                send(slab, slabs.at[i, own_rows], xsend_sem, xrecv_sem.at[i],
                     (z, y, lax.rem(x + dx, NX), core))
        slab = acts.at[block_of(i, 1 - c)]
        send(slab, slabs.at[i, own_rows], xsend_sem, xrecv_sem.at[i], (z, y, x, 1 - c))
        return carry

    lax.fori_loop(0, STEPS, gather_step, 0)

    wait_bytes(slabs.at[:, pl.ds(0, 64)], own_sem)
    wait_bytes(cols.at[:, pl.ds(0, 256)], swap_recv)

    def multiply(i):
        wait_bytes(slabs.at[i, pl.ds(0, 448)], xrecv_sem.at[i])
        part[i % 2] = lax.dot_general(
            slabs[i], cols[...], (((0,), (0,)), ((), ())), preferred_element_type=jnp.float32
        )
        for k in range(1, NY):
            rows = pl.ds(pl.multiple_of(lax.rem(y + k, NY) * 32, 32), 32)
            piece = part[i % 2, rows, :].astype(jnp.bfloat16)
            for core in range(NC):
                for which in range(2):
                    at = core * 256 + which * 128
                    ysend[i, k - 1, core, which * 32 : which * 32 + 32, :] = piece[:, at : at + 128]
        for k in range(1, NY):
            send(ysend.at[i, k - 1], yrecv.at[i, k - 1], ysend_sem, yrecv_sem.at[i], at_y(k))

    def pass_on(i):
        wait_bytes(yrecv.at[i], yrecv_sem.at[i])
        rows = pl.ds(pl.multiple_of(y * 32, 32), 32)
        for core in range(NC):
            for which in range(2):
                at = core * 256 + which * 128
                total = part[i % 2, rows, at : at + 128]
                for k in range(NY - 1):
                    total += yrecv[i, k, core, which * 32 : which * 32 + 32, :].astype(jnp.float32)
                zsend[i, core, which * 32 : which * 32 + 32, :] = total.astype(jnp.bfloat16)
        k = jnp.where(c == 0, 8 + i, 7 - i)

        @pl.when(k != 0)
        def _():
            send(zsend.at[i], zrecv.at[i], zsend_sem, zrecv_sem.at[i], at_z(k))

    multiply(0)

    def reduce_step(i, carry):
        multiply(i)
        pass_on(i - 1)
        return carry

    lax.fori_loop(1, STEPS, reduce_step, 0)
    pass_on(STEPS - 1)

    for core in range(NC):
        half[core] = jnp.zeros((64, 128), jnp.float32)

    def collect(i):
        wait_bytes(zrecv.at[i], zrecv_sem.at[i])
        for core in range(NC):
            half[core] += zrecv[i, core].astype(jnp.float32)

    for i in range(STEPS - 1):
        collect(i)

    @pl.when(c == 0)
    def _():
        collect(STEPS - 1)

    @pl.when(c == 1)
    def _():
        for core in range(NC):
            half[core] += zsend[STEPS - 1, core].astype(jnp.float32)

    send(half.at[1 - c], peer_half, half_send, half_recv, at_group(0, 1))
    wait_bytes(peer_half, half_recv)

    tokens = 64 * NX * NC * NZ * NY
    gradient = (half[c] + peer_half[...]) * (1.0 / tokens)

    squares = jnp.sum(gradient * gradient, axis=0, keepdims=True)
    nsend[0] = squares
    for n, (dx, dc) in enumerate(GROUP):
        send(nsend.at[0], nrecv_g.at[n], nsend_sem.at[0], nrecv_sem.at[0], at_group(dx, dc))
    wait_bytes(nrecv_g, nrecv_sem.at[0])
    for n in range(len(GROUP)):
        squares += nrecv_g[n]
    nsend[1] = squares
    for k in range(1, NY):
        send(nsend.at[1], nrecv_y.at[k - 1], nsend_sem.at[1], nrecv_sem.at[1], at_y(k))
    wait_bytes(nrecv_y, nrecv_sem.at[1])
    for k in range(NY - 1):
        squares += nrecv_y[k]
    nsend[2] = squares
    for k in (8, 7, 9, 6, 10, 5, 11, 4, 12, 3, 13, 2, 14, 1, 15):
        send(nsend.at[2], nrecv_z.at[k - 1], nsend_sem.at[2], nrecv_sem.at[2], at_z(k))
    for n in range(3):
        wait_bytes((master, first, second)[n], state_sem.at[n])
    wait_bytes(nrecv_z, nrecv_sem.at[2])
    for k in range(NZ - 1):
        squares += nrecv_z[k]

    grad_norm = jnp.sqrt(jnp.sum(squares, axis=1, keepdims=True))
    limit = clip_scale * math.sqrt(2.0 * D * KV)
    clip_factor = jnp.minimum(jnp.float32(1.0), limit / (grad_norm + 1e-06))
    clipped_all = clip_factor * gradient
    for which in range(2):
        pick = pl.ds(which, 32, stride=2)
        clipped = clipped_all[which * 32 : which * 32 + 32]
        weights = master[pick, :]
        m = beta_first * first[pick, :] + (1.0 - beta_first) * clipped
        v = beta_second * second[pick, :] + (1.0 - beta_second) * clipped * clipped
        first_hat = m / (1.0 - beta_first**STEP)
        second_hat = v / (1.0 - beta_second**STEP)
        new = weights - learning_rate * (
            first_hat / (jnp.sqrt(second_hat) + adam_epsilon) + weight_decay * weights
        )
        rows_out[0, pick, :] = new
        rows_out[1, pick, :] = m
        rows_out[2, pick, :] = v
    wbuf[dp] = rows_out[0].astype(jnp.bfloat16)

    own = wbuf.at[dp]
    for n, k in enumerate((8, 7, 9, 6, 10, 5, 11, 4, 12, 3, 13, 2, 14, 1, 15)):
        send(own, own, gsend_sem, gz_sem.at[n], at_z(k))
    for k in range(1, NY):
        send(own, own, gsend_sem, gy_sem, at_y(k))
    for n, out in enumerate((master_out, first_out, second_out)):
        pltpu.make_async_copy(rows_out.at[n], out, out_sem.at[n]).start()
    for n, k in enumerate((8, 7, 9, 6, 10, 5, 11, 4, 12, 3, 13, 2, 14, 1, 15)):
        got = wbuf.at[lax.rem(z + NZ - k, NZ) * NY + y]
        wait_bytes(got, gz_sem.at[n])
        for k_y in range(1, NY):
            send(got, got, gsend_sem, gy_sem, at_y(k_y))
    wait_bytes(wbuf.at[pl.ds(0, 48)], gy_sem)
    pltpu.make_async_copy(wbuf, weights_out, out_sem.at[3]).start()

    wait_bytes(cols.at[:, pl.ds(0, 256)], swap_send)
    wait_bytes(slabs.at[pl.ds(0, 7)], xsend_sem)
    wait_bytes(yrecv, ysend_sem)
    wait_bytes(zsend.at[pl.ds(0, 7)], zsend_sem)

    @pl.when(c == 0)
    def _():
        wait_bytes(zsend.at[7], zsend_sem)

    wait_bytes(peer_half, half_send)
    wait_bytes(nrecv_g, nsend_sem.at[0])
    wait_bytes(nrecv_y, nsend_sem.at[1])
    wait_bytes(nrecv_z, nsend_sem.at[2])
    wait_bytes(wbuf.at[pl.ds(0, 63)], gsend_sem)
    for n in range(3):
        pltpu.make_async_copy(rows_out.at[n], (master_out, first_out, second_out)[n], out_sem.at[n]).wait()
    pltpu.make_async_copy(wbuf, weights_out, out_sem.at[3]).wait()


def on_device(activations, key_value_grads, master_weights, first_moment, second_moment):
    f32, bf16 = jnp.float32, jnp.bfloat16
    any_space = pl.BlockSpec(memory_space=pl.ANY)
    dma = pltpu.SemaphoreType.DMA
    vmem = pltpu.VMEM
    flat = [a.reshape(64, 128) for a in (master_weights, first_moment, second_moment)]
    outs = pl.pallas_call(
        step_kernel,
        out_shape=[jax.ShapeDtypeStruct((64, 128), f32)] * 3 + [jax.ShapeDtypeStruct((64, 64, 128), bf16)],
        in_specs=[any_space] * 5,
        out_specs=[any_space] * 4,
        scratch_shapes=[
            vmem((NZ, 64, 128), bf16),
            vmem((STEPS, 512, 128), bf16),
            vmem((512, 512), bf16),
            vmem((2, 128, 512), f32),
            vmem((STEPS, NY - 1, NC, 64, 128), bf16),
            vmem((STEPS, NY - 1, NC, 64, 128), bf16),
            vmem((STEPS, NC, 64, 128), bf16),
            vmem((STEPS, NC, 64, 128), bf16),
            vmem((NC, 64, 128), f32),
            vmem((64, 128), f32),
            vmem((3, 1, 128), f32),
            vmem((len(GROUP), 1, 128), f32),
            vmem((NY - 1, 1, 128), f32),
            vmem((NZ - 1, 1, 128), f32),
            vmem((64, 128), f32),
            vmem((64, 128), f32),
            vmem((64, 128), f32),
            vmem((64, 128), f32),
            vmem((3, 64, 128), f32),
            vmem((64, 64, 128), bf16),
            dma, dma, dma, dma((3,)), dma, dma,
            dma, dma((STEPS,)), dma, dma((STEPS,)), dma, dma((STEPS,)),
            dma, dma, dma((3,)), dma((3,)), dma, dma((NZ - 1,)), dma, dma((4,)),
        ],
        compiler_params=pltpu.CompilerParams(collective_id=0, has_side_effects=True),
        name="adam_step",
    )(activations, key_value_grads, *flat)
    return tuple(o.reshape(32, 2, 128) for o in outs[:3]) + (outs[3].reshape(D, 2, 128),)


def solution(mesh):
    split = Mesh(mesh.devices.reshape(NZ, NY, NX, NC), DP_MP)
    return jax.shard_map(
        on_device,
        mesh=split,
        in_specs=(
            P(DP_MP, None),
            P(None, DP, MP),
            P(DP, None, MP),
            P(DP, None, MP),
            P(DP, None, MP),
        ),
        out_specs=(P(DP, None, MP), P(DP, None, MP), P(DP, None, MP), P(None, None, MP)),
        check_vma=False,
    )
```

time: 228 us -> 83.1 us (0.36)
  blocking collectives: 139 us -> 0 us
  Pallas kernels: 0 us -> 76.7 us
  waiting for transfers between devices: 58.3 us -> 0 us
  between operations: 14.9 us -> 0.65 us
  local copies, waits for them, and re-layouts: 10.1 us -> 5.34 us
  matrix products: 2.3 us -> 0 us
    all_to_all x6 -> x0, blocking collectives: 127 us -> none  [the longest x4 53.8 us: copy_for_each(): lax.all_to_all(jnp.broadcast_to(x[None], (count, *x.shape)), axis, 0, 0,...]
    pallas_call x0 -> x1, Pallas kernels: none -> 76.7 us  [on_device(): pl.pallas_call(step_kernel, out_shape=[jax.ShapeDtypeStruct((64, 128), f3...]
    all_gather x1 -> x0, waiting for transfers between devices: 58.3 us -> none  [gather_axes(): result = lax.all_gather(result, axes[number], axis=dim, tiled=True)]
    all_gather x1 -> x0, blocking collectives: 12.6 us -> none  [gather_axes(): result = lax.all_gather(result, axes[number], axis=dim, tiled=True)]
    broadcast_in_dim x4 -> x0, local copies, waits for them, and re-layouts: 2.66 us -> none  [copy_for_each(): jnp.broadcast_to(x[None], (count, *x.shape))]
    dot_general x1 -> x0, local copies, waits for them, and re-layouts: 2.52 us -> none  [on_device(): jnp.einsum('td,ctk->dck', gathered_by_axis(activations, ('mp_0', 'mp_1'),...]
    dot_general x1 -> x0, matrix products: 2.3 us -> none  [on_device(): jnp.einsum('td,ctk->dck', gathered_by_axis(activations, ('mp_0', 'mp_1'),...]
    unnamed x12 -> x8, local copies, waits for them, and re-layouts: 4.51 us -> 5.34 us
  transfers between devices with their start and end apart: 1 -> 0, of which waited for: 1 -> 0; matrix products, arithmetic and copies ran while one was open for 1% -> 0% of each run, Pallas kernels for 0% -> 0%
where the time goes in v1:
time: 83.1 us; the launch traced here: 82.7 us
  Pallas kernels  76.7 us (92%)
  local copies, waits for them, and re-layouts  5.34 us (6%)
    pallas_call x1, Pallas kernels, on_device(): pl.pallas_call(step_kernel, out_shape=[jax.ShapeDtypeStruct((64, 128), f3...  76.7 us
    unnamed x8, local copies, waits for them, and re-layouts  5.34 us

profile of v1, /device:TPU:6, one launch (start us, length us, event | category | flops | bytes accessed | tf_op | source)
XLA Modules:
  0.0 82.7 jit_solution(8694003819867265624)
XLA Ops:
  0.6 76.7 %adam_step.1 = (f32[64,128]{1,0:T(8,128)}, f32[64,128]{1,0:T(8,128)}, f32[64,128]{1,0:T(8,128)}, bf16[64,64,128]{2,1,0:T(8,128)(2,1)}) custom-call(bf16[64,2048]{1,0:T(8,128)(2,1)} %acts_hbm.1, bf16[2,512,128]{2,1,0:T(8,128)(2,1)} %grads_hbm.1, f32[64,128]{1,0:T(8,128)} %bitcast.8, f32[64,128]{1,0:T(8,128)} %bitcast.9, f32[64,128]{1,0:T(8,128)} %bitcast.10), custom_call_target="tpu_custom_call" | custom-call | tf_op jit(solution)/shard_map/adam_step/pallas_call | solution.py:259
  77.4 0.0 copy-start.1
  77.4 1.4 %copy.13 = f32[32,2,128]{2,1,0:T(2,128)} copy(f32[32,2,128]{2,1,0:T(2,128)} %bitcast.13) | data formatting | bytes 65536
  78.8 0.0 copy-done.1
  78.8 0.0 copy-start
  78.8 0.6 copy.14
  79.4 0.2 copy-done
  79.5 0.6 copy.15
  80.1 2.6 %copy.16 = bf16[2048,2,128]{2,1,0:T(2,128)(2,1)} copy(bf16[2048,2,128]{2,1,0:T(2,128)(2,1)} %bitcast.7) | data formatting | bytes 2097152
Async XLA Ops:
  77.4 1.4 %copy-start.1 = (f32[64,128]{1,0:T(8,128)S(1)}, f32[64,128]{1,0:T(8,128)}, u32[]{:S(2)}) copy-start(f32[64,128]{1,0:T(8,128)} %get-tuple-element.9) | copy-start | bytes 98308
  78.8 0.8 copy-start

commit v2 on v1

v2 whole, which is shorter than its diff:
```python
import math

import jax
import jax.numpy as jnp
from jax import lax
from jax.experimental import pallas as pl
from jax.experimental.pallas import tpu as pltpu
from jax.sharding import Mesh
from jax.sharding import PartitionSpec as P

D = 2048
STEP = 8
KV = 1024
NZ, NY, NX, NC = 16, 4, 4, 2
STEPS = 8
AHEAD = 3
LAG = 2
PARTS = LAG + 1
DP = ("z", "y")
MP = ("x", "c")
DP_MP = ("z", "y", "x", "c")
MESH_ID = pl.DeviceIdType.MESH

beta_first = 0.9
beta_second = 0.95
adam_epsilon = 1e-08
learning_rate = 0.001
weight_decay = 0.1
clip_scale = 0.001

PLANE = [(dy, dx, dc) for dy in range(NY) for dx in range(NX) for dc in range(NC) if (dy, dx, dc) != (0, 0, 0)]
Z_ORDER = (8, 7, 9, 6, 10, 5, 11, 4, 12, 3, 13, 2, 14, 1, 15)
SPREAD = (4, -4, 1, -1, 2, -2, 3, -3)
ARRIVAL = (1, -1, 4, -4, 2, -2, 3, -3, 5, -5, 6, -6, 7, -7, 8)


def step_kernel(
    acts_hbm, grads_hbm, master_hbm, first_hbm, second_hbm,
    master_out, first_out, second_out, wbuf,
    acts, slabs, cols, part, ysend, yrecv, zsend, zrecv,
    nsend, nrecv_p, nrecv_z,
    master, first, second,
    load_sem, own_sem, grad_sem, state_sem, swap_send, swap_recv,
    xsend_sem, xrecv_sem, ysend_sem, yrecv_sem, zsend_sem, zrecv_sem,
    nsend_sem, nrecv_sem, gsend_sem, gz_sem, gy_sem,
):
    z, y, x, c = (lax.axis_index(a) for a in DP_MP)
    dp = z * NY + y
    mp = x * NC + c

    def at_z(k):
        return (lax.rem(z + k, NZ), y, x, c)

    def at_y(k):
        return (z, lax.rem(y + k, NY), x, c)

    def in_plane(dy, dx, dc):
        return (z, lax.rem(y + dy, NY), lax.rem(x + dx, NX), lax.rem(c + dc, NC))

    def block_of(i, core):
        return lax.rem(z + jnp.where(core == 0, 8 + i, 7 - i), NZ)

    def send(src, dst, send_sem, recv_sem, device):
        copy = pltpu.make_async_remote_copy(
            src_ref=src, dst_ref=dst, send_sem=send_sem, recv_sem=recv_sem,
            device_id=device, device_id_type=MESH_ID,
        )
        copy.start()

    def wait_bytes(ref, sem):
        pltpu.make_async_copy(ref, ref, sem).wait()

    barrier = pltpu.get_barrier_semaphore()
    for k in Z_ORDER:
        for core in range(NC):
            pl.semaphore_signal(barrier, inc=1, device_id=(lax.rem(z + k, NZ), y, x, core), device_id_type=MESH_ID)
    for d in PLANE:
        pl.semaphore_signal(barrier, inc=1, device_id=in_plane(*d), device_id_type=MESH_ID)

    own_rows = pl.ds(pl.multiple_of(mp * 64, 64), 64)
    own_cols = pl.ds(pl.multiple_of(c * 256, 256), 256)
    for b in range(NZ):
        pltpu.make_async_copy(acts_hbm.at[:, pl.ds(b * 128, 128)], acts.at[b], load_sem).start()
    for which in range(2):
        lanes = pl.ds(pl.multiple_of(c * 256 + which * 128, 128), 128)
        pltpu.make_async_copy(grads_hbm.at[which], cols.at[:, lanes], grad_sem).start()
    for i in range(STEPS):
        lanes = pl.ds(pl.multiple_of(block_of(i, c) * 128, 128), 128)
        pltpu.make_async_copy(acts_hbm.at[:, lanes], slabs.at[i, own_rows], own_sem).start()
    pltpu.make_async_copy(master_hbm, master, state_sem.at[0]).start()
    pltpu.make_async_copy(first_hbm, first, state_sem.at[1]).start()
    pltpu.make_async_copy(second_hbm, second, state_sem.at[2]).start()

    wait_bytes(acts, load_sem)
    wait_bytes(cols.at[:, pl.ds(0, 256)], grad_sem)
    pl.semaphore_wait(barrier, NC * (NZ - 1) + len(PLANE))

    send(cols.at[:, own_cols], cols.at[:, own_cols], swap_send, swap_recv, in_plane(0, 0, 1))

    def gather_step(i):
        for core in range(NC):
            slab = acts.at[block_of(i, core)]
            for dx in range(1, NX):
                send(slab, slabs.at[i, own_rows], xsend_sem, xrecv_sem.at[i],
                     (z, y, lax.rem(x + dx, NX), core))
        slab = acts.at[block_of(i, 1 - c)]
        send(slab, slabs.at[i, own_rows], xsend_sem, xrecv_sem.at[i], (z, y, x, 1 - c))

    for i in range(AHEAD):
        gather_step(i)

    wait_bytes(slabs.at[:, pl.ds(0, 64)], own_sem)
    wait_bytes(cols.at[:, pl.ds(0, 256)], swap_recv)

    def multiply(i):
        wait_bytes(slabs.at[i, pl.ds(0, 448)], xrecv_sem.at[i])

        @pl.when(i + AHEAD < STEPS)
        def _():
            gather_step(i + AHEAD)

        part[i % PARTS] = lax.dot_general(
            slabs[i], cols[...], (((0,), (0,)), ((), ())), preferred_element_type=jnp.float32
        )
        for k in range(1, NY):
            rows = pl.ds(pl.multiple_of(lax.rem(y + k, NY) * 32, 32), 32)
            piece = part[i % PARTS, rows, :].astype(jnp.bfloat16)
            for core in range(NC):
                for which in range(2):
                    at = core * 256 + which * 128
                    ysend[i, k - 1, core, which * 32 : which * 32 + 32, :] = piece[:, at : at + 128]
        for k in range(1, NY):
            send(ysend.at[i, k - 1], yrecv.at[i, k - 1], ysend_sem, yrecv_sem.at[i], at_y(k))

    def pass_on(i):
        wait_bytes(yrecv.at[i], yrecv_sem.at[i])
        rows = pl.ds(pl.multiple_of(y * 32, 32), 32)
        for core in range(NC):
            for which in range(2):
                at = core * 256 + which * 128
                total = part[i % PARTS, rows, at : at + 128]
                for k in range(NY - 1):
                    total += yrecv[i, k, core, which * 32 : which * 32 + 32, :].astype(jnp.float32)
                zsend[i, core, which * 32 : which * 32 + 32, :] = total.astype(jnp.bfloat16)
        k = jnp.where(c == 0, 8 + i, 7 - i)

        slot = 2 * i + c
        send(zsend.at[i, 0], zrecv.at[slot], zsend_sem, zrecv_sem.at[slot], (lax.rem(z + k, NZ), y, x, 0))

        @pl.when(k != 0)
        def _():
            send(zsend.at[i, 1], zrecv.at[slot], zsend_sem, zrecv_sem.at[slot], (lax.rem(z + k, NZ), y, x, 1))

    for i in range(LAG):
        multiply(i)

    def reduce_step(i, carry):
        multiply(i)
        pass_on(i - LAG)
        return carry

    lax.fori_loop(LAG, STEPS, reduce_step, 0)
    for i in range(STEPS - LAG, STEPS):
        pass_on(i)

    @pl.when(c == 1)
    def _():
        zrecv[NZ - 1] = zsend[STEPS - 1, 1]

    @pl.when(c == 0)
    def _():
        wait_bytes(zrecv.at[NZ - 1], zrecv_sem.at[NZ - 1])

    total = jnp.zeros((64, 128), jnp.float32)
    for slot in range(NZ - 1):
        wait_bytes(zrecv.at[slot], zrecv_sem.at[slot])
        total += zrecv[slot].astype(jnp.float32)
    total += zrecv[NZ - 1].astype(jnp.float32)

    tokens = 64 * NX * NC * NZ * NY
    gradient = total * (1.0 / tokens)

    squares = jnp.sum(gradient * gradient, axis=0, keepdims=True)
    nsend[0] = squares
    for n, d in enumerate(PLANE):
        send(nsend.at[0], nrecv_p.at[n], nsend_sem.at[0], nrecv_sem.at[0], in_plane(*d))
    wait_bytes(nrecv_p, nrecv_sem.at[0])
    squares += jnp.sum(nrecv_p[...], axis=0)
    nsend[1] = squares
    for k in Z_ORDER:
        send(nsend.at[1], nrecv_z.at[k - 1], nsend_sem.at[1], nrecv_sem.at[1], at_z(k))
    for n in range(3):
        wait_bytes((master, first, second)[n], state_sem.at[n])
    wait_bytes(nrecv_z, nrecv_sem.at[1])
    squares += jnp.sum(nrecv_z[...], axis=0)

    grad_norm = jnp.sqrt(jnp.sum(squares, axis=1, keepdims=True))
    limit = clip_scale * math.sqrt(2.0 * D * KV)
    clip_factor = jnp.minimum(jnp.float32(1.0), limit / (grad_norm + 1e-06))
    clipped_all = clip_factor * gradient
    for which in range(2):
        pick = pl.ds(which, 32, stride=2)
        clipped = clipped_all[which * 32 : which * 32 + 32]
        weights = master[pick, :]
        m = beta_first * first[pick, :] + (1.0 - beta_first) * clipped
        v = beta_second * second[pick, :] + (1.0 - beta_second) * clipped * clipped
        first_hat = m / (1.0 - beta_first**STEP)
        second_hat = v / (1.0 - beta_second**STEP)
        new = weights - learning_rate * (
            first_hat / (jnp.sqrt(second_hat) + adam_epsilon) + weight_decay * weights
        )
        master_out[pick, :] = new
        first_out[pick, :] = m
        second_out[pick, :] = v
    wbuf[dp] = master_out[...].astype(jnp.bfloat16)

    own = wbuf.at[dp]
    side = jnp.where(c == 0, 1, NZ - 1)

    def along(k):
        return lax.rem(z + side * (k + NZ), NZ)

    def pass_along(block, k, by):
        send(block, block, gsend_sem, gz_sem.at[ARRIVAL.index(k)], (along(by), y, x, c))

    def pass_across(block):
        for k in range(1, NY):
            send(block, block, gsend_sem, gy_sem, at_y(k))

    for k in SPREAD:
        pass_along(own, k, k)
    pass_across(own)
    for n, k in enumerate(ARRIVAL):
        got = wbuf.at[along(-k) * NY + y]
        wait_bytes(got, gz_sem.at[n])
        if k == 4:
            for by in (4, 3, 2, 1):
                pass_along(got, 4 + by, by)
        if k == -4:
            for by in (3, 2, 1):
                pass_along(got, -4 - by, -by)
        pass_across(got)
    wait_bytes(wbuf.at[pl.ds(0, 48)], gy_sem)

    wait_bytes(cols.at[:, pl.ds(0, 256)], swap_send)
    wait_bytes(slabs.at[pl.ds(0, 7)], xsend_sem)
    wait_bytes(yrecv, ysend_sem)
    wait_bytes(zrecv.at[pl.ds(0, NZ - 1)], zsend_sem)

    @pl.when(c == 0)
    def _():
        wait_bytes(zrecv.at[NZ - 1], zsend_sem)

    wait_bytes(nrecv_p, nsend_sem.at[0])
    wait_bytes(nrecv_z, nsend_sem.at[1])
    wait_bytes(wbuf.at[pl.ds(0, 63)], gsend_sem)


def write_kernel(*refs):
    ins, outs, sem = refs[:4], refs[4:8], refs[8]
    copies = [pltpu.make_async_copy(i, o, sem.at[n]) for n, (i, o) in enumerate(zip(ins, outs))]
    for copy in copies:
        copy.start()
    for copy in copies:
        copy.wait()


def on_device(activations, key_value_grads, master_weights, first_moment, second_moment):
    f32, bf16 = jnp.float32, jnp.bfloat16
    any_space = pl.BlockSpec(memory_space=pl.ANY)
    dma = pltpu.SemaphoreType.DMA
    vmem = pltpu.VMEM
    flat = [a.reshape(64, 128) for a in (master_weights, first_moment, second_moment)]
    in_vmem = pl.BlockSpec(memory_space=pltpu.VMEM)
    results = pl.pallas_call(
        step_kernel,
        out_shape=[vmem((64, 128), f32)] * 3 + [vmem((64, 64, 128), bf16)],
        in_specs=[any_space] * 5,
        out_specs=[in_vmem] * 4,
        scratch_shapes=[
            vmem((NZ, 64, 128), bf16),
            vmem((STEPS, 512, 128), bf16),
            vmem((512, 512), bf16),
            vmem((PARTS, 128, 512), f32),
            vmem((STEPS, NY - 1, NC, 64, 128), bf16),
            vmem((STEPS, NY - 1, NC, 64, 128), bf16),
            vmem((STEPS, NC, 64, 128), bf16),
            vmem((NZ, 64, 128), bf16),
            vmem((2, 1, 128), f32),
            vmem((len(PLANE), 1, 128), f32),
            vmem((NZ - 1, 1, 128), f32),
            vmem((64, 128), f32),
            vmem((64, 128), f32),
            vmem((64, 128), f32),
            dma, dma, dma, dma((3,)), dma, dma,
            dma, dma((STEPS,)), dma, dma((STEPS,)), dma, dma((NZ,)),
            dma((2,)), dma((2,)), dma, dma((NZ - 1,)), dma,
        ],
        compiler_params=pltpu.CompilerParams(collective_id=0, has_side_effects=True),
        name="adam_step",
    )(activations, key_value_grads, *flat)
    results = [pltpu.with_memory_space_constraint(r, pltpu.VMEM) for r in results]
    outs = pl.pallas_call(
        write_kernel,
        out_shape=[jax.ShapeDtypeStruct((64, 128), f32)] * 3 + [jax.ShapeDtypeStruct((64, 64, 128), bf16)],
        in_specs=[any_space] * 4,
        out_specs=[any_space] * 4,
        scratch_shapes=[dma((4,))],
        name="write_out",
    )(*results)
    return tuple(o.reshape(32, 2, 128) for o in outs[:3]) + (outs[3].reshape(D, 2, 128),)


def solution(mesh):
    split = Mesh(mesh.devices.reshape(NZ, NY, NX, NC), DP_MP)
    return jax.shard_map(
        on_device,
        mesh=split,
        in_specs=(
            P(DP_MP, None),
            P(None, DP, MP),
            P(DP, None, MP),
            P(DP, None, MP),
            P(DP, None, MP),
        ),
        out_specs=(P(DP, None, MP), P(DP, None, MP), P(DP, None, MP), P(None, None, MP)),
        check_vma=False,
    )
```

time: 83.1 us -> 68.6 us (0.83)
  Pallas kernels: 76.7 us -> 67.7 us
  local copies, waits for them, and re-layouts: 5.34 us -> 0 us
    pallas_call x1 -> x2, Pallas kernels: 76.7 us -> 67.7 us  [the longest x1 66.7 us: on_device(): pl.pallas_call(step_kernel, out_shape=[vmem((64, 128), f32)] * 3 + [vmem(...]
    unnamed x8 -> x0, local copies, waits for them, and re-layouts: 5.34 us -> none
where the time goes in v2:
time: 68.6 us; the launch traced here: 68.4 us
  Pallas kernels  67.7 us (99%)
    pallas_call x1, Pallas kernels, on_device(): pl.pallas_call(step_kernel, out_shape=[vmem((64, 128), f32)] * 3 + [vmem(...  66.7 us

profile of v2, /device:TPU:6, one launch (start us, length us, event | category | flops | bytes accessed | tf_op | source)
XLA Modules:
  0.0 68.4 jit_solution(9543464152299370328)
XLA Ops:
  0.6 66.7 %adam_step.1 = (f32[64,128]{1,0:T(8,128)S(1)}, f32[64,128]{1,0:T(8,128)S(1)}, f32[64,128]{1,0:T(8,128)S(1)}, bf16[64,64,128]{2,1,0:T(8,128)(2,1)S(1)}) custom-call(bf16[64,2048]{1,0:T(8,128)(2,1)} %acts_hbm.1, bf16[2,512,128]{2,1,0:T(8,128)(2,1)} %grads_hbm.1, f32[64,128]{1,0:T(8,128)} %bitcast.7, f32[64,128]{1,0:T(8,128)} %bitcast.8, f32[64,128]{1,0:T(8,128)} %bitcast.9), custom_call_target="tpu_custom_call" | custom-call | tf_op jit(solution)/shard_map/adam_step/pallas_call | solution.py:275
  67.3 1.0 %write_out.1 = (f32[64,128]{1,0:T(8,128)}, f32[64,128]{1,0:T(8,128)}, f32[64,128]{1,0:T(8,128)}, bf16[64,64,128]{2,1,0:T(8,128)(2,1)}) custom-call(f32[64,128]{1,0:T(8,128)S(1)} %get-tuple-element.12.refs_0_, f32[64,128]{1,0:T(8,128)S(1)} %get-tuple-element.13.refs_1_, f32[64,128]{1,0:T(8,128)S(1)} %get-tuple-element.14.refs_2_, ...), custom_call_target="tpu_custom_call" | custom-call | tf_op jit(solution)/shard_map/write_out/pallas_call | solution.py:303

commit v3 on v2

--- a/solution.py
+++ b/solution.py
@@ -28,7 +28,7 @@
 weight_decay = 0.1
 clip_scale = 0.001
 
-PLANE = [(dy, dx, dc) for dy in range(NY) for dx in range(NX) for dc in range(NC) if (dy, dx, dc) != (0, 0, 0)]
+PLANE = NY * NX * NC
 Z_ORDER = (8, 7, 9, 6, 10, 5, 11, 4, 12, 3, 13, 2, 14, 1, 15)
 SPREAD = (4, -4, 1, -1, 2, -2, 3, -3)
 ARRIVAL = (1, -1, 4, -4, 2, -2, 3, -3, 5, -5, 6, -6, 7, -7, 8)
@@ -42,7 +42,7 @@
     master, first, second,
     load_sem, own_sem, grad_sem, state_sem, swap_send, swap_recv,
     xsend_sem, xrecv_sem, ysend_sem, yrecv_sem, zsend_sem, zrecv_sem,
-    nsend_sem, nrecv_sem, gsend_sem, gz_sem, gy_sem,
+    nsend_sem, nrecv_sem, gsend_sem, gz_sem, gy_sem, known,
 ):
     z, y, x, c = (lax.axis_index(a) for a in DP_MP)
     dp = z * NY + y
@@ -71,11 +71,11 @@
         pltpu.make_async_copy(ref, ref, sem).wait()
 
     barrier = pltpu.get_barrier_semaphore()
-    for k in Z_ORDER:
-        for core in range(NC):
-            pl.semaphore_signal(barrier, inc=1, device_id=(lax.rem(z + k, NZ), y, x, core), device_id_type=MESH_ID)
-    for d in PLANE:
-        pl.semaphore_signal(barrier, inc=1, device_id=in_plane(*d), device_id_type=MESH_ID)
+    near = [in_plane(0, dx, dc) for dx in range(NX) for dc in range(NC) if (dx, dc) != (0, 0)]
+    near += [at_y(k) for k in range(1, NY)]
+    near += [(lax.rem(z + k, NZ), y, x, core) for k in (1, NZ - 1) for core in range(NC)]
+    for device in near:
+        pl.semaphore_signal(barrier, inc=1, device_id=device, device_id_type=MESH_ID)
 
     own_rows = pl.ds(pl.multiple_of(mp * 64, 64), 64)
     own_cols = pl.ds(pl.multiple_of(c * 256, 256), 256)
@@ -93,7 +93,13 @@
 
     wait_bytes(acts, load_sem)
     wait_bytes(cols.at[:, pl.ds(0, 256)], grad_sem)
-    pl.semaphore_wait(barrier, NC * (NZ - 1) + len(PLANE))
+    pl.semaphore_wait(barrier, len(near))
+
+    def tell(level, devices):
+        for device in devices:
+            pl.semaphore_signal(known.at[level], inc=1, device_id=device, device_id_type=MESH_ID)
+
+    tell(0, [at_y(k) for k in range(1, NY)] + [at_z(1), at_z(NZ - 1)])
 
     send(cols.at[:, own_cols], cols.at[:, own_cols], swap_send, swap_recv, in_plane(0, 0, 1))
 
@@ -109,6 +115,8 @@
     for i in range(AHEAD):
         gather_step(i)
 
+    pl.semaphore_wait(known.at[0], NY + 1)
+    tell(1, [at_z(2), at_z(NZ - 2)])
     wait_bytes(slabs.at[:, pl.ds(0, 64)], own_sem)
     wait_bytes(cols.at[:, pl.ds(0, 256)], swap_recv)
 
@@ -151,8 +159,12 @@
         def _():
             send(zsend.at[i, 1], zrecv.at[slot], zsend_sem, zrecv_sem.at[slot], (lax.rem(z + k, NZ), y, x, 1))
 
-    for i in range(LAG):
+    multiply(0)
+    pl.semaphore_wait(known.at[1], 2)
+    tell(2, [at_z(4), at_z(NZ - 4)])
+    for i in range(1, LAG):
         multiply(i)
+    pl.semaphore_wait(known.at[2], 2)
 
     def reduce_step(i, carry):
         multiply(i)
@@ -182,17 +194,39 @@
 
     squares = jnp.sum(gradient * gradient, axis=0, keepdims=True)
     nsend[0] = squares
-    for n, d in enumerate(PLANE):
-        send(nsend.at[0], nrecv_p.at[n], nsend_sem.at[0], nrecv_sem.at[0], in_plane(*d))
-    wait_bytes(nrecv_p, nrecv_sem.at[0])
-    squares += jnp.sum(nrecv_p[...], axis=0)
-    nsend[1] = squares
-    for k in Z_ORDER:
-        send(nsend.at[1], nrecv_z.at[k - 1], nsend_sem.at[1], nrecv_sem.at[1], at_z(k))
+    for dy in range(NY):
+        for dx in range(NX):
+            slot = nrecv_p.at[(dy * NX + dx) * NC + c]
+            if (dy, dx) != (0, 0):
+                send(nsend.at[0], slot, nsend_sem.at[0], nrecv_sem.at[0], (z, lax.rem(y + dy, NY), lax.rem(x + dx, NX), 1))
+
+    @pl.when(c == 0)
+    def _():
+        send(nsend.at[0], nrecv_p.at[0], nsend_sem.at[0], nrecv_sem.at[0], (z, y, x, 1))
+
+    @pl.when(c == 1)
+    def _():
+        nrecv_p[1] = squares
+        wait_bytes(nrecv_p.at[pl.ds(0, PLANE - 1)], nrecv_sem.at[0])
+        plane_sum = jnp.sum(nrecv_p[...], axis=0)
+        nsend[1] = plane_sum
+        nrecv_z[0] = plane_sum
+        for k in Z_ORDER:
+            for core in range(NC):
+                send(nsend.at[1], nrecv_z.at[k], nsend_sem.at[1], nrecv_sem.at[1], (lax.rem(z + k, NZ), y, x, core))
+        send(nsend.at[1], nrecv_z.at[0], nsend_sem.at[1], nrecv_sem.at[1], (z, y, x, 0))
+
     for n in range(3):
         wait_bytes((master, first, second)[n], state_sem.at[n])
-    wait_bytes(nrecv_z, nrecv_sem.at[1])
-    squares += jnp.sum(nrecv_z[...], axis=0)
+    @pl.when(c == 0)
+    def _():
+        wait_bytes(nrecv_z, nrecv_sem.at[1])
+
+    @pl.when(c == 1)
+    def _():
+        wait_bytes(nrecv_z.at[pl.ds(1, NZ - 1)], nrecv_sem.at[1])
+
+    squares = jnp.sum(nrecv_z[...], axis=0)
 
     grad_norm = jnp.sqrt(jnp.sum(squares, axis=1, keepdims=True))
     limit = clip_scale * math.sqrt(2.0 * D * KV)
@@ -251,8 +285,16 @@
     def _():
         wait_bytes(zrecv.at[NZ - 1], zsend_sem)
 
-    wait_bytes(nrecv_p, nsend_sem.at[0])
-    wait_bytes(nrecv_z, nsend_sem.at[1])
+    wait_bytes(nrecv_p.at[pl.ds(0, NY * NX - 1)], nsend_sem.at[0])
+
+    @pl.when(c == 0)
+    def _():
+        wait_bytes(nrecv_p.at[0], nsend_sem.at[0])
+
+    @pl.when(c == 1)
+    def _():
+        wait_bytes(nrecv_p.at[pl.ds(0, NC * NZ - 1)], nsend_sem.at[1])
+
     wait_bytes(wbuf.at[pl.ds(0, 63)], gsend_sem)
 
 
@@ -287,14 +329,15 @@
             vmem((STEPS, NC, 64, 128), bf16),
             vmem((NZ, 64, 128), bf16),
             vmem((2, 1, 128), f32),
-            vmem((len(PLANE), 1, 128), f32),
-            vmem((NZ - 1, 1, 128), f32),
+            vmem((PLANE, 1, 128), f32),
+            vmem((NZ, 1, 128), f32),
             vmem((64, 128), f32),
             vmem((64, 128), f32),
             vmem((64, 128), f32),
             dma, dma, dma, dma((3,)), dma, dma,
             dma, dma((STEPS,)), dma, dma((STEPS,)), dma, dma((NZ,)),
             dma((2,)), dma((2,)), dma, dma((NZ - 1,)), dma,
+            pltpu.SemaphoreType.REGULAR((3,)),
         ],
         compiler_params=pltpu.CompilerParams(collective_id=0, has_side_effects=True),
         name="adam_step",

time: 68.6 us -> 66.1 us (0.964)
  Pallas kernels: 67.7 us -> 65 us
    pallas_call x1, Pallas kernels: 66.7 us -> 64 us  [on_device(): pl.pallas_call(step_kernel, out_shape=[vmem((64, 128), f32)] * 3 + [vmem(...]
where the time goes in v3:
time: 66.1 us; the launch traced here: 65.6 us
  Pallas kernels  65 us (98%)
    pallas_call x1, Pallas kernels, on_device(): pl.pallas_call(step_kernel, out_shape=[vmem((64, 128), f32)] * 3 + [vmem(...  64 us

profile of v3, /device:TPU:6, one launch (start us, length us, event | category | flops | bytes accessed | tf_op | source)
XLA Modules:
  0.0 65.6 jit_solution(13973738216588715031)
XLA Ops:
  0.6 64.0 %adam_step.1 = (f32[64,128]{1,0:T(8,128)S(1)}, f32[64,128]{1,0:T(8,128)S(1)}, f32[64,128]{1,0:T(8,128)S(1)}, bf16[64,64,128]{2,1,0:T(8,128)(2,1)S(1)}) custom-call(bf16[64,2048]{1,0:T(8,128)(2,1)} %acts_hbm.1, bf16[2,512,128]{2,1,0:T(8,128)(2,1)} %grads_hbm.1, f32[64,128]{1,0:T(8,128)} %bitcast.7, f32[64,128]{1,0:T(8,128)} %bitcast.8, f32[64,128]{1,0:T(8,128)} %bitcast.9), custom_call_target="tpu_custom_call" | custom-call | tf_op jit(solution)/shard_map/adam_step/pallas_call | solution.py:317
  64.6 1.0 %write_out.1 = (f32[64,128]{1,0:T(8,128)}, f32[64,128]{1,0:T(8,128)}, f32[64,128]{1,0:T(8,128)}, bf16[64,64,128]{2,1,0:T(8,128)(2,1)}) custom-call(f32[64,128]{1,0:T(8,128)S(1)} %get-tuple-element.12.refs_0_, f32[64,128]{1,0:T(8,128)S(1)} %get-tuple-element.13.refs_1_, f32[64,128]{1,0:T(8,128)S(1)} %get-tuple-element.14.refs_2_, ...), custom_call_target="tpu_custom_call" | custom-call | tf_op jit(solution)/shard_map/write_out/pallas_call | solution.py:346

commit v4 on v3

--- a/solution.py
+++ b/solution.py
@@ -13,7 +13,7 @@
 KV = 1024
 NZ, NY, NX, NC = 16, 4, 4, 2
 STEPS = 8
-AHEAD = 3
+AHEAD = 8
 LAG = 2
 PARTS = LAG + 1
 DP = ("z", "y")
@@ -28,20 +28,23 @@
 weight_decay = 0.1
 clip_scale = 0.001
 
-PLANE = NY * NX * NC
+PLANE = [(dy, dx) for dy in (2, 1, 3, 0) for dx in (2, 1, 3, 0) if (dy, dx) != (0, 0)]
 Z_ORDER = (8, 7, 9, 6, 10, 5, 11, 4, 12, 3, 13, 2, 14, 1, 15)
-SPREAD = (4, -4, 1, -1, 2, -2, 3, -3)
+ONWARD = {0: (4, -4, 1, -1, 2, -2, 3, -3), 4: (8, 7, 6, 5), -4: (-7, -6, -5)}
 ARRIVAL = (1, -1, 4, -4, 2, -2, 3, -3, 5, -5, 6, -6, 7, -7, 8)
+ACROSS = (2, 1, 3)
+YSENDS = (2, 1, 3)
+XSENDS = (2, 1, 3)
 
 
 def step_kernel(
     acts_hbm, grads_hbm, master_hbm, first_hbm, second_hbm,
     master_out, first_out, second_out, wbuf,
     acts, slabs, cols, part, ysend, yrecv, zsend, zrecv,
-    nsend, nrecv_p, nrecv_z,
-    master, first, second,
+    nsend, nrecv_p, nrecv_z, nsum,
+    state, gsum, half,
     load_sem, own_sem, grad_sem, state_sem, swap_send, swap_recv,
-    xsend_sem, xrecv_sem, ysend_sem, yrecv_sem, zsend_sem, zrecv_sem,
+    xsend_sem, xrecv_sem, ysend_sem, yrecv_sem, zsend_sem, zrecv_sem, half_send, half_recv,
     nsend_sem, nrecv_sem, gsend_sem, gz_sem, gy_sem, known,
 ):
     z, y, x, c = (lax.axis_index(a) for a in DP_MP)
@@ -87,9 +90,8 @@
     for i in range(STEPS):
         lanes = pl.ds(pl.multiple_of(block_of(i, c) * 128, 128), 128)
         pltpu.make_async_copy(acts_hbm.at[:, lanes], slabs.at[i, own_rows], own_sem).start()
-    pltpu.make_async_copy(master_hbm, master, state_sem.at[0]).start()
-    pltpu.make_async_copy(first_hbm, first, state_sem.at[1]).start()
-    pltpu.make_async_copy(second_hbm, second, state_sem.at[2]).start()
+    for n, ref in enumerate((master_hbm, first_hbm, second_hbm)):
+        pltpu.make_async_copy(ref, state.at[n], state_sem).start()
 
     wait_bytes(acts, load_sem)
     wait_bytes(cols.at[:, pl.ds(0, 256)], grad_sem)
@@ -106,7 +108,7 @@
     def gather_step(i):
         for core in range(NC):
             slab = acts.at[block_of(i, core)]
-            for dx in range(1, NX):
+            for dx in XSENDS:
                 send(slab, slabs.at[i, own_rows], xsend_sem, xrecv_sem.at[i],
                      (z, y, lax.rem(x + dx, NX), core))
         slab = acts.at[block_of(i, 1 - c)]
@@ -118,6 +120,7 @@
     pl.semaphore_wait(known.at[0], NY + 1)
     tell(1, [at_z(2), at_z(NZ - 2)])
     wait_bytes(slabs.at[:, pl.ds(0, 64)], own_sem)
+    wait_bytes(state, state_sem)
     wait_bytes(cols.at[:, pl.ds(0, 256)], swap_recv)
 
     def multiply(i):
@@ -137,7 +140,7 @@
                 for which in range(2):
                     at = core * 256 + which * 128
                     ysend[i, k - 1, core, which * 32 : which * 32 + 32, :] = piece[:, at : at + 128]
-        for k in range(1, NY):
+        for k in YSENDS:
             send(ysend.at[i, k - 1], yrecv.at[i, k - 1], ysend_sem, yrecv_sem.at[i], at_y(k))
 
     def pass_on(i):
@@ -153,16 +156,14 @@
         k = jnp.where(c == 0, 8 + i, 7 - i)
 
         slot = 2 * i + c
-        send(zsend.at[i, 0], zrecv.at[slot], zsend_sem, zrecv_sem.at[slot], (lax.rem(z + k, NZ), y, x, 0))
 
         @pl.when(k != 0)
         def _():
-            send(zsend.at[i, 1], zrecv.at[slot], zsend_sem, zrecv_sem.at[slot], (lax.rem(z + k, NZ), y, x, 1))
-
-    multiply(0)
+            send(zsend.at[i], zrecv.at[slot], zsend_sem, zrecv_sem.at[slot], (lax.rem(z + k, NZ), y, x, 1))
+
     pl.semaphore_wait(known.at[1], 2)
     tell(2, [at_z(4), at_z(NZ - 4)])
-    for i in range(1, LAG):
+    for i in range(LAG):
         multiply(i)
     pl.semaphore_wait(known.at[2], 2)
 
@@ -175,80 +176,72 @@
     for i in range(STEPS - LAG, STEPS):
         pass_on(i)
 
+    def clip(sums):
+        grad_norm = jnp.sqrt(jnp.sum(sums, axis=1, keepdims=True))
+        limit = clip_scale * math.sqrt(2.0 * D * KV)
+        return jnp.minimum(jnp.float32(1.0), limit / (grad_norm + 1e-06))
+
+    def adam(gradient, clip_factor, held, new_out, first_to, second_to):
+        clipped_all = clip_factor * gradient
+        for which in range(2):
+            pick = pl.ds(which, 32, stride=2)
+            clipped = clipped_all[which * 32 : which * 32 + 32]
+            weights = held[0, pick, :]
+            m = beta_first * held[1, pick, :] + (1.0 - beta_first) * clipped
+            v = beta_second * held[2, pick, :] + (1.0 - beta_second) * clipped * clipped
+            first_hat = m / (1.0 - beta_first**STEP)
+            second_hat = v / (1.0 - beta_second**STEP)
+            new_out[pick, :] = weights - learning_rate * (
+                first_hat / (jnp.sqrt(second_hat) + adam_epsilon) + weight_decay * weights
+            )
+            if first_to is not None:
+                first_to[pick, :] = m
+                second_to[pick, :] = v
+
+    scale = 1.0 / (64 * NX * NC * NZ * NY)
+
+    @pl.when(c == 0)
+    def _():
+        wait_bytes(gsum, half_recv)
+        wait_bytes(nrecv_z, nrecv_sem.at[1])
+        factor = clip(jnp.sum(nrecv_z[...], axis=0))
+        adam(gsum[...], factor, state, master_out, first_out, second_out)
+        wait_bytes(zrecv.at[pl.ds(0, STEPS)], zsend_sem)
+
     @pl.when(c == 1)
     def _():
-        zrecv[NZ - 1] = zsend[STEPS - 1, 1]
-
-    @pl.when(c == 0)
-    def _():
-        wait_bytes(zrecv.at[NZ - 1], zrecv_sem.at[NZ - 1])
-
-    total = jnp.zeros((64, 128), jnp.float32)
-    for slot in range(NZ - 1):
-        wait_bytes(zrecv.at[slot], zrecv_sem.at[slot])
-        total += zrecv[slot].astype(jnp.float32)
-    total += zrecv[NZ - 1].astype(jnp.float32)
-
-    tokens = 64 * NX * NC * NZ * NY
-    gradient = total * (1.0 / tokens)
-
-    squares = jnp.sum(gradient * gradient, axis=0, keepdims=True)
-    nsend[0] = squares
-    for dy in range(NY):
-        for dx in range(NX):
-            slot = nrecv_p.at[(dy * NX + dx) * NC + c]
-            if (dy, dx) != (0, 0):
-                send(nsend.at[0], slot, nsend_sem.at[0], nrecv_sem.at[0], (z, lax.rem(y + dy, NY), lax.rem(x + dx, NX), 1))
-
-    @pl.when(c == 0)
-    def _():
-        send(nsend.at[0], nrecv_p.at[0], nsend_sem.at[0], nrecv_sem.at[0], (z, y, x, 1))
-
-    @pl.when(c == 1)
-    def _():
-        nrecv_p[1] = squares
-        wait_bytes(nrecv_p.at[pl.ds(0, PLANE - 1)], nrecv_sem.at[0])
+        totals = [zsend[STEPS - 1, core].astype(jnp.float32) for core in range(NC)]
+        for slot in range(NZ - 1):
+            wait_bytes(zrecv.at[slot], zrecv_sem.at[slot])
+            for core in range(NC):
+                totals[core] += zrecv[slot, core].astype(jnp.float32)
+        gradients = [total * scale for total in totals]
+        squares = jnp.sum(gradients[0] * gradients[0] + gradients[1] * gradients[1], axis=0, keepdims=True)
+        nsend[0] = squares
+        nrecv_p[0] = squares
+        for dy, dx in PLANE:
+            send(nsend.at[0], nrecv_p.at[dy * NX + dx], nsend_sem.at[0], nrecv_sem.at[0],
+                 (z, lax.rem(y + dy, NY), lax.rem(x + dx, NX), 1))
+        half[...] = gradients[0]
+        gsum[...] = gradients[1]
+        send(half, gsum, half_send, half_recv, (z, y, x, 0))
+        wait_bytes(nrecv_p.at[pl.ds(1, NY * NX - 1)], nrecv_sem.at[0])
         plane_sum = jnp.sum(nrecv_p[...], axis=0)
         nsend[1] = plane_sum
         nrecv_z[0] = plane_sum
-        for k in Z_ORDER:
-            for core in range(NC):
+        for core in (1, 0):
+            for k in Z_ORDER:
                 send(nsend.at[1], nrecv_z.at[k], nsend_sem.at[1], nrecv_sem.at[1], (lax.rem(z + k, NZ), y, x, core))
         send(nsend.at[1], nrecv_z.at[0], nsend_sem.at[1], nrecv_sem.at[1], (z, y, x, 0))
-
-    for n in range(3):
-        wait_bytes((master, first, second)[n], state_sem.at[n])
-    @pl.when(c == 0)
-    def _():
-        wait_bytes(nrecv_z, nrecv_sem.at[1])
-
-    @pl.when(c == 1)
-    def _():
         wait_bytes(nrecv_z.at[pl.ds(1, NZ - 1)], nrecv_sem.at[1])
-
-    squares = jnp.sum(nrecv_z[...], axis=0)
-
-    grad_norm = jnp.sqrt(jnp.sum(squares, axis=1, keepdims=True))
-    limit = clip_scale * math.sqrt(2.0 * D * KV)
-    clip_factor = jnp.minimum(jnp.float32(1.0), limit / (grad_norm + 1e-06))
-    clipped_all = clip_factor * gradient
-    for which in range(2):
-        pick = pl.ds(which, 32, stride=2)
-        clipped = clipped_all[which * 32 : which * 32 + 32]
-        weights = master[pick, :]
-        m = beta_first * first[pick, :] + (1.0 - beta_first) * clipped
-        v = beta_second * second[pick, :] + (1.0 - beta_second) * clipped * clipped
-        first_hat = m / (1.0 - beta_first**STEP)
-        second_hat = v / (1.0 - beta_second**STEP)
-        new = weights - learning_rate * (
-            first_hat / (jnp.sqrt(second_hat) + adam_epsilon) + weight_decay * weights
-        )
-        master_out[pick, :] = new
-        first_out[pick, :] = m
-        second_out[pick, :] = v
+        factor = clip(jnp.sum(nrecv_z[...], axis=0))
+        adam(gsum[...], factor, state, master_out, first_out, second_out)
+        wait_bytes(zrecv.at[pl.ds(0, STEPS - 1)], zsend_sem)
+        wait_bytes(half, half_send)
+        wait_bytes(nrecv_p.at[pl.ds(1, NY * NX - 1)], nsend_sem.at[0])
+        wait_bytes(nsum.at[pl.ds(0, NC * NZ - 1)], nsend_sem.at[1])
+
     wbuf[dp] = master_out[...].astype(jnp.bfloat16)
-
-    own = wbuf.at[dp]
     side = jnp.where(c == 0, 1, NZ - 1)
 
     def along(k):
@@ -258,44 +251,24 @@
         send(block, block, gsend_sem, gz_sem.at[ARRIVAL.index(k)], (along(by), y, x, c))
 
     def pass_across(block):
-        for k in range(1, NY):
+        for k in ACROSS:
             send(block, block, gsend_sem, gy_sem, at_y(k))
 
-    for k in SPREAD:
+    own = wbuf.at[dp]
+    for k in ONWARD[0]:
         pass_along(own, k, k)
     pass_across(own)
     for n, k in enumerate(ARRIVAL):
         got = wbuf.at[along(-k) * NY + y]
         wait_bytes(got, gz_sem.at[n])
-        if k == 4:
-            for by in (4, 3, 2, 1):
-                pass_along(got, 4 + by, by)
-        if k == -4:
-            for by in (3, 2, 1):
-                pass_along(got, -4 - by, -by)
+        for further in ONWARD.get(k, ()):
+            pass_along(got, further, further - k)
         pass_across(got)
     wait_bytes(wbuf.at[pl.ds(0, 48)], gy_sem)
-
+    wait_bytes(wbuf.at[pl.ds(0, 63)], gsend_sem)
     wait_bytes(cols.at[:, pl.ds(0, 256)], swap_send)
     wait_bytes(slabs.at[pl.ds(0, 7)], xsend_sem)
     wait_bytes(yrecv, ysend_sem)
-    wait_bytes(zrecv.at[pl.ds(0, NZ - 1)], zsend_sem)
-
-    @pl.when(c == 0)
-    def _():
-        wait_bytes(zrecv.at[NZ - 1], zsend_sem)
-
-    wait_bytes(nrecv_p.at[pl.ds(0, NY * NX - 1)], nsend_sem.at[0])
-
-    @pl.when(c == 0)
-    def _():
-        wait_bytes(nrecv_p.at[0], nsend_sem.at[0])
-
-    @pl.when(c == 1)
-    def _():
-        wait_bytes(nrecv_p.at[pl.ds(0, NC * NZ - 1)], nsend_sem.at[1])
-
-    wait_bytes(wbuf.at[pl.ds(0, 63)], gsend_sem)
 
 
 def write_kernel(*refs):
@@ -327,15 +300,16 @@
             vmem((STEPS, NY - 1, NC, 64, 128), bf16),
             vmem((STEPS, NY - 1, NC, 64, 128), bf16),
             vmem((STEPS, NC, 64, 128), bf16),
-            vmem((NZ, 64, 128), bf16),
+            vmem((NZ, NC, 64, 128), bf16),
             vmem((2, 1, 128), f32),
-            vmem((PLANE, 1, 128), f32),
+            vmem((NY * NX, 1, 128), f32),
             vmem((NZ, 1, 128), f32),
+            vmem((NZ * NC, 1, 128), f32),
+            vmem((3, 64, 128), f32),
             vmem((64, 128), f32),
             vmem((64, 128), f32),
-            vmem((64, 128), f32),
-            dma, dma, dma, dma((3,)), dma, dma,
-            dma, dma((STEPS,)), dma, dma((STEPS,)), dma, dma((NZ,)),
+            dma, dma, dma, dma, dma, dma,
+            dma, dma((STEPS,)), dma, dma((STEPS,)), dma, dma((NZ,)), dma, dma,
             dma((2,)), dma((2,)), dma, dma((NZ - 1,)), dma,
             pltpu.SemaphoreType.REGULAR((3,)),
         ],

time: 66.1 us -> 65 us (0.983)
  Pallas kernels: 65 us -> 64.1 us
    pallas_call x1, Pallas kernels: 64 us -> 63 us  [on_device(): pl.pallas_call(step_kernel, out_shape=[vmem((64, 128), f32)] * 3 + [vmem(...]
where the time goes in v4:
time: 65 us; the launch traced here: 64.7 us
  Pallas kernels  64.1 us (99%)
    pallas_call x1, Pallas kernels, on_device(): pl.pallas_call(step_kernel, out_shape=[vmem((64, 128), f32)] * 3 + [vmem(...  63 us

profile of v4, /device:TPU:6, one launch (start us, length us, event | category | flops | bytes accessed | tf_op | source)
XLA Modules:
  0.0 64.7 jit_solution(18192974231933214449)
XLA Ops:
  0.6 63.0 %adam_step.1 = (f32[64,128]{1,0:T(8,128)S(1)}, f32[64,128]{1,0:T(8,128)S(1)}, f32[64,128]{1,0:T(8,128)S(1)}, bf16[64,64,128]{2,1,0:T(8,128)(2,1)S(1)}) custom-call(bf16[64,2048]{1,0:T(8,128)(2,1)} %acts_hbm.1, bf16[2,512,128]{2,1,0:T(8,128)(2,1)} %grads_hbm.1, f32[64,128]{1,0:T(8,128)} %bitcast.7, f32[64,128]{1,0:T(8,128)} %bitcast.8, f32[64,128]{1,0:T(8,128)} %bitcast.9), custom_call_target="tpu_custom_call" | custom-call | tf_op jit(solution)/shard_map/adam_step/pallas_call | solution.py:290
  63.7 1.0 %write_out.1 = (f32[64,128]{1,0:T(8,128)}, f32[64,128]{1,0:T(8,128)}, f32[64,128]{1,0:T(8,128)}, bf16[64,64,128]{2,1,0:T(8,128)(2,1)}) custom-call(f32[64,128]{1,0:T(8,128)S(1)} %get-tuple-element.12.refs_0_, f32[64,128]{1,0:T(8,128)S(1)} %get-tuple-element.13.refs_1_, f32[64,128]{1,0:T(8,128)S(1)} %get-tuple-element.14.refs_2_, ...), custom_call_target="tpu_custom_call" | custom-call | tf_op jit(solution)/shard_map/write_out/pallas_call | solution.py:320

commit v5 on v4

--- a/solution.py
+++ b/solution.py
@@ -15,6 +15,7 @@
 STEPS = 8
 AHEAD = 8
 LAG = 2
+SWAP_AT = 2
 PARTS = LAG + 1
 DP = ("z", "y")
 MP = ("x", "c")
@@ -94,7 +95,6 @@
         pltpu.make_async_copy(ref, state.at[n], state_sem).start()
 
     wait_bytes(acts, load_sem)
-    wait_bytes(cols.at[:, pl.ds(0, 256)], grad_sem)
     pl.semaphore_wait(barrier, len(near))
 
     def tell(level, devices):
@@ -103,7 +103,6 @@
 
     tell(0, [at_y(k) for k in range(1, NY)] + [at_z(1), at_z(NZ - 1)])
 
-    send(cols.at[:, own_cols], cols.at[:, own_cols], swap_send, swap_recv, in_plane(0, 0, 1))
 
     def gather_step(i):
         for core in range(NC):
@@ -115,6 +114,9 @@
         send(slab, slabs.at[i, own_rows], xsend_sem, xrecv_sem.at[i], (z, y, x, 1 - c))
 
     for i in range(AHEAD):
+        if i == SWAP_AT:
+            wait_bytes(cols.at[:, pl.ds(0, 256)], grad_sem)
+            send(cols.at[:, own_cols], cols.at[:, own_cols], swap_send, swap_recv, in_plane(0, 0, 1))
         gather_step(i)
 
     pl.semaphore_wait(known.at[0], NY + 1)
@@ -229,8 +231,8 @@
         plane_sum = jnp.sum(nrecv_p[...], axis=0)
         nsend[1] = plane_sum
         nrecv_z[0] = plane_sum
-        for core in (1, 0):
-            for k in Z_ORDER:
+        for k in Z_ORDER:
+            for core in (0, 1):
                 send(nsend.at[1], nrecv_z.at[k], nsend_sem.at[1], nrecv_sem.at[1], (lax.rem(z + k, NZ), y, x, core))
         send(nsend.at[1], nrecv_z.at[0], nsend_sem.at[1], nrecv_sem.at[1], (z, y, x, 0))
         wait_bytes(nrecv_z.at[pl.ds(1, NZ - 1)], nrecv_sem.at[1])

time: 65 us -> 64.9 us (level)
  no operation moved by 1% of the time
where the time goes in v5:
time: 64.9 us; the launch traced here: 64.7 us
  Pallas kernels  64.1 us (99%)
    pallas_call x1, Pallas kernels, on_device(): pl.pallas_call(step_kernel, out_shape=[vmem((64, 128), f32)] * 3 + [vmem(...  63.1 us

profile of v5, /device:TPU:6, one launch (start us, length us, event | category | flops | bytes accessed | tf_op | source)
XLA Modules:
  0.0 64.7 jit_solution(9468228990079901174)
XLA Ops:
  0.6 63.1 %adam_step.1 = (f32[64,128]{1,0:T(8,128)S(1)}, f32[64,128]{1,0:T(8,128)S(1)}, f32[64,128]{1,0:T(8,128)S(1)}, bf16[64,64,128]{2,1,0:T(8,128)(2,1)S(1)}) custom-call(bf16[64,2048]{1,0:T(8,128)(2,1)} %acts_hbm.1, bf16[2,512,128]{2,1,0:T(8,128)(2,1)} %grads_hbm.1, f32[64,128]{1,0:T(8,128)} %bitcast.7, f32[64,128]{1,0:T(8,128)} %bitcast.8, f32[64,128]{1,0:T(8,128)} %bitcast.9), custom_call_target="tpu_custom_call" | custom-call | tf_op jit(solution)/shard_map/adam_step/pallas_call | solution.py:292
  63.7 1.0 %write_out.1 = (f32[64,128]{1,0:T(8,128)}, f32[64,128]{1,0:T(8,128)}, f32[64,128]{1,0:T(8,128)}, bf16[64,64,128]{2,1,0:T(8,128)(2,1)}) custom-call(f32[64,128]{1,0:T(8,128)S(1)} %get-tuple-element.12.refs_0_, f32[64,128]{1,0:T(8,128)S(1)} %get-tuple-element.13.refs_1_, f32[64,128]{1,0:T(8,128)S(1)} %get-tuple-element.14.refs_2_, ...), custom_call_target="tpu_custom_call" | custom-call | tf_op jit(solution)/shard_map/write_out/pallas_call | solution.py:322
